TPU v7x, 256 devices: a whole 4x4x8 slice. The times are simulated.
256 devices in a mesh: prow: 16 (over z, core), pcol: 16 (over x, y).
Axes of the slice: x: 4, y: 4, z: 8, core: 2. Of those that a mesh axis runs over, the one named last changes fastest.
Arguments:
- inv_lead: float32 [4, 16, 256, 4, 16, 256], P(None, 'prow', None, None, 'pcol'), may hold values from -1 to 2, as said below
- h_lead: float32 [4, 16, 256, 6, 16, 256], P(None, 'pcol', None, None, 'prow'), may hold values from -6 to 6
- h_slab: float32 [512, 6, 16, 256], P('pcol', None, 'prow'), may hold values from -6 to 6
- l_panel: float32 [512, 4, 16, 256], P('pcol', None, 'prow'), may hold values from -0.046875 to 0.046875
- l_diag: float32 [512, 512], replicated, may hold values from -1 to 2, as said below
Outputs:
- x_slab: float32 [512, 6, 16, 256], P('pcol', None, 'prow')
- y_lead: float32 [512, 4, 16, 256], P('pcol', None, 'prow')
- y_diag: float32 [512, 512], P('pcol', 'prow')
Inputs may be any that keep to these rules, and one draw needn't show every extreme that they name: inv_lead is lower triangular in natural order, with diagonal entries between 1 and 2. l_diag is lower triangular, with diagonal entries between 1 and 2.
All inputs are finite; a program needn't handle non-finite values.
Results may differ from a plain program's by a relative error of at most 0.00018.
Values sent between devices are 32-bit elements; how exact they have to be, the bound alone decides.
No kernel may reach another device: no remote copies, remote signals or barrier semaphores. Data moves between devices by JAX's collectives and lax.ppermute only.
A program may use at most 128 MiB of HBM per device.

v0:
```python
import jax
import jax.numpy as jnp
from jax import lax
from jax.sharding import PartitionSpec as P


def copy_for_each(value, axis):
    copies = jnp.broadcast_to(value, (lax.axis_size(axis), *value.shape))
    return lax.all_to_all(copies, axis, split_axis=0, concat_axis=0, tiled=True)


def joined_along(parts, dim):
    lengths = list(parts.shape[1:])
    lengths[dim] *= parts.shape[0]
    return jnp.moveaxis(parts, 0, dim).reshape(lengths)


def gathered_copies(value, axis, dim):
    parts = copy_for_each(value, axis)
    return joined_along(parts, dim)


def in_blocks(value, dim, size):
    lengths = value.shape
    parts = value.reshape(*lengths[:dim], size, lengths[dim] // size, *lengths[dim + 1 :])
    return jnp.moveaxis(parts, dim, 0)


def sum_at_owner(value, axis, dim):
    parts = in_blocks(value, dim, lax.axis_size(axis))
    arrived = lax.all_to_all(parts, axis, split_axis=0, concat_axis=0, tiled=True)
    return arrived.sum(axis=0)


def in_one_piece(arrays, axis, dim, along):
    widths = [a.shape[along] for a in arrays]
    both = jnp.concatenate(arrays, axis=along)
    result = lax.psum_scatter(both, axis, scatter_dimension=dim, tiled=True)
    return tuple(jnp.split(result, [sum(widths[:k]) for k in range(1, len(widths))], axis=along))


def matmul_hi(left, right):
    return jnp.dot(left, right, precision=lax.Precision.HIGHEST, preferred_element_type=jnp.float32)


def matmul_trans(left, right):
    return lax.dot_general(
        left,
        right,
        (((1,), (1,)), ((), ())),
        precision=lax.Precision.HIGHEST,
        preferred_element_type=jnp.float32,
    )


def invert_diag(l_diag, block_size):
    diag_top = l_diag[:block_size, :block_size]
    diag_bottom = l_diag[block_size:, block_size:]
    off_block = l_diag[block_size:, :block_size]
    identity = jnp.eye(block_size, dtype=jnp.float32)
    top_inv = lax.linalg.triangular_solve(diag_top, identity, left_side=True, lower=True)
    bottom_inv = lax.linalg.triangular_solve(diag_bottom, identity, left_side=True, lower=True)
    corner = -matmul_hi(bottom_inv, matmul_hi(off_block, top_inv))
    upper_rows = jnp.concatenate([top_inv, jnp.zeros_like(top_inv)], axis=1)
    lower_rows = jnp.concatenate([corner, bottom_inv], axis=1)
    return jnp.concatenate([upper_rows, lower_rows], axis=0)


def per_device(inv_lead, h_lead, h_slab, l_panel, l_diag):
    slab_rows = l_diag.shape[0]
    block_size = l_panel.shape[3]
    prev_blocks = l_panel.shape[1]
    x_rows = l_panel.shape[0]
    h_blocks = h_slab.shape[1]
    diag_inv = invert_diag(l_diag, slab_rows // 2)
    inv_local = inv_lead.reshape(prev_blocks * block_size, -1)
    col_width = inv_local.shape[1]
    col_blocks = col_width // block_size
    h_local = h_lead.reshape(col_width, -1)
    h_side = h_slab.reshape(x_rows, -1)
    y_rows = slab_rows // lax.axis_size("prow")
    row_start = lax.axis_index("prow") * y_rows
    col_start = lax.axis_index("pcol") * x_rows
    piece = gathered_copies(l_panel, "pcol", 0)
    factor = matmul_hi(diag_inv, piece.reshape(piece.shape[0], -1))
    side_term = matmul_hi(lax.dynamic_slice_in_dim(diag_inv, col_start, x_rows, 1), h_side)
    own_panel = sum_at_owner(-matmul_hi(factor, inv_local), "prow", 0)
    product = matmul_hi(lax.all_gather(own_panel, "prow", axis=0, tiled=True), h_local)
    x_local = sum_at_owner(product + side_term, "pcol", 0)
    x_slab = x_local.reshape(x_rows, h_blocks, 1, block_size)
    kept_cols = x_slab[:, : prev_blocks + 1]
    widened = lax.all_gather(kept_cols, "prow", axis=2, tiled=True).reshape(x_rows, -1)
    prev_rows = prev_blocks * block_size * lax.axis_size("prow")
    head_cols = widened[:, :prev_rows]
    tail_cols = widened[:, prev_rows : prev_rows + slab_rows]
    shifted_x = lax.all_to_all(
        head_cols.reshape(x_rows, col_blocks, lax.axis_size("pcol"), block_size),
        "pcol",
        split_axis=2,
        concat_axis=0,
        tiled=True,
    )
    shifted_x = shifted_x.reshape(slab_rows, col_width)
    lead_part = matmul_trans(shifted_x, inv_local)
    diag_part = matmul_trans(shifted_x, own_panel)
    y_first, y_block = in_one_piece((lead_part, diag_part), "pcol", 0, 1)
    diag_rows = lax.dynamic_slice_in_dim(diag_inv, row_start, y_rows, 0)
    y_diag = y_block + matmul_trans(tail_cols, diag_rows)
    return (x_slab, y_first.reshape(x_rows, prev_blocks, 1, block_size), y_diag)


def solution(mesh):
    return jax.shard_map(
        per_device,
        mesh=mesh,
        in_specs=(
            P(None, "prow", None, None, "pcol", None),
            P(None, "pcol", None, None, "prow", None),
            P("pcol", None, "prow", None),
            P("pcol", None, "prow", None),
            P(),
        ),
        out_specs=(P("pcol", None, "prow", None), P("pcol", None, "prow", None), P("pcol", "prow")),
        check_vma=False,
    )
```

profile of v0, /device:TPU:2, one launch (start us, length us, event | category | flops | bytes accessed | tf_op | source)
XLA Modules:
  0.0 457.1 jit_solution(1383191247335577584)
XLA Ops:
  8.1 2.9 broadcast_in_dim.4
  11.1 7.5 %all-to-all-start = ((f32[16,32,4,1,256]{4,3,2,1,0:T(1,128)}), f32[16,32,4,1,256]{4,3,2,1,0:T(1,128)S(1)}, u32[]{:S(2)}, u32[]{:S(2)}) async-start(f32[16,32,4,1,256]{4,3,2,1,0:T(1,128)} %broadcast_in_dim.4), calls=%async_computation | async-start | bytes 4194304 | tf_op jit(solution)/shard_map/all_to_all | solution.py:9
  19.8 3.8 while.4
  23.6 19.7 %custom-call.4 = f32[2,128,128]{1,2,0:T(8,128)S(1)} custom-call(f32[2,128,128]{2,1,0:T(8,128)S(1)} %get-tuple-element.18), custom_call_target="InvertDiagBlocksLowerTriangular" | custom-call | tf_op jit(solution)/shard_map/triangular_solve/custom-call.1 | solution.py:61
  43.3 4.0 while.5
  47.3 19.7 %custom-call.5 = f32[2,128,128]{1,2,0:T(8,128)S(1)} custom-call(f32[2,128,128]{2,1,0:T(8,128)S(1)} %get-tuple-element.19), custom_call_target="InvertDiagBlocksLowerTriangular" | custom-call | tf_op jit(solution)/shard_map/triangular_solve/custom-call.1 | solution.py:62
  67.0 14.2 %reduce.1 = f32[4,256,4,256]{3,2,1,0:T(4,128)} reduce(f32[4,1,256,4,1,256]{5,4,3,2,1,0:T(1,128)} %param.7, f32[]{:T(128)} %constant.47), dimensions={1,4}, to_apply=%param.7.reduce_sub_computation | reduce | bytes 8388612 | tf_op args[0]
  81.2 5.2 %copy.34 = f32[128,8,4,256]{3,1,2,0:T(8,128)} copy(f32[128,8,4,256]{3,2,1,0:T(4,128)} %bitcast.82) | data formatting | bytes 8388608
  90.2 7.4 %reduce = f32[16,32,4,256]{3,2,1,0:T(4,128)} reduce(f32[16,32,4,1,256]{4,3,2,1,0:T(1,128)S(1)} %all-to-all-done, f32[]{:T(128)} %constant.47), dimensions={3}, to_apply=%all_to_all.20.reduce_sub_computation | reduce | bytes 4194308 | tf_op jit(solution)/shard_map/all_to_all | solution.py:9
  97.6 2.1 copy.33
  99.7 4.0 fusion.22
  103.7 6.9 %convolution_negate_fusion = f32[512,1024]{1,0:T(8,128)S(1)} fusion(f32[512,1024]{1,0:T(8,128)S(1)} %fusion.22, f32[1024,1024]{1,0:T(8,128)S(1)} %bitcast.77), kind=kOutput, calls=%fused_computation.6 | convolution fusion | flops 6442975232 | bytes 8388608 | tf_op jit(solution)/shard_map/dot_general | solution.py:43
  110.6 58.0 %all_to_all.31 = f32[16,32,1024]{2,1,0:T(8,128)S(1)} all-to-all(f32[16,32,1024]{2,1,0:T(8,128)S(1)} %bitcast.92), channel_id=1, replica_groups=mesh['prow'=16,'pcol'=16] {'prow'}, dimensions={0} | all-to-all | bytes 4194304 | tf_op jit(solution)/shard_map/all_to_all | solution.py:31
  169.5 37.4 %reduce.2 = f32[4,256,6,256]{3,2,1,0:T(8,128)} reduce(f32[4,1,256,6,1,256]{5,4,3,2,1,0:T(1,128)} %param.8, f32[]{:T(128)} %constant.47), dimensions={1,4}, to_apply=%param.8.reduce_sub_computation | reduce | bytes 12582916 | tf_op args[1]
  206.8 9.2 %copy.35 = f32[128,8,6,256]{3,1,2,0:T(8,128)} copy(f32[128,8,6,256]{3,2,1,0:T(8,128)} %bitcast.79) | data formatting | bytes 12582912
  216.8 13.7 %fusion.25 = f32[512,1536]{1,0:T(8,128)S(1)} fusion(f32[512,1024]{1,0:T(8,128)} %all-gather.3.cloned.1.call-done, f32[1024,1536]{1,0:T(8,128)} %bitcast.93), kind=kOutput, calls=%fused_computation.47 | convolution fusion | flops 9663676416 | bytes 11534336 | tf_op jit(solution)/shard_map/dot_general | solution.py:43
  230.4 2.8 convolution_add_fusion
  233.2 45.1 %all_to_all.32 = f32[16,32,1536]{2,1,0:T(8,128)S(1)} all-to-all(f32[16,32,1536]{2,1,0:T(8,128)S(1)} %bitcast.83), channel_id=1, replica_groups=mesh['prow'=16,'pcol'=16] {'pcol'}, dimensions={0} | all-to-all | bytes 6291456 | tf_op jit(solution)/shard_map/all_to_all | solution.py:31
  279.4 36.6 %all-gather.5.cloned.1.call-done = f32[32,5,16,256]{3,0,1,2:T(8,128)} async-done(((f32[32,5,1,256]{3,0,1,2:T(8,128)}), f32[32,5,16,256]{3,0,1,2:T(8,128)}) %all-gather.5.cloned.1.call-update) | async-done | bytes 2621456 | tf_op jit(solution)/shard_map/all_gather | solution.py:92
  315.9 3.3 copy.25
  322.9 33.8 %all_to_all.30 = f32[32,4,16,256]{3,1,0,2:T(4,128)S(1)} all-to-all(f32[32,4,16,256]{3,1,0,2:T(4,128)S(1)} %copy.26), channel_id=1, replica_groups=mesh['prow'=16,'pcol'=16] {'pcol'}, dimensions={2} | all-to-all | bytes 4194304 | tf_op jit(solution)/shard_map/all_to_all | solution.py:96
  358.8 7.0 %fusion.26 = f32[512,1024]{1,0:T(8,128)S(1)} fusion(f32[512,1024]{1,0:T(8,128)S(1)} %bitcast.80, f32[1024,1024]{1,0:T(8,128)S(1)} %bitcast.78), kind=kOutput, calls=%fused_computation.48 | convolution fusion | flops 6442450944 | bytes 8388608 | tf_op jit(solution)/shard_map/dot_general | solution.py:47
  365.8 1.8 fusion.27
  370.1 76.6 %reduce-scatter.2.cloned.1.call-done = f32[32,1056]{1,0:T(8,128)} async-done(((f32[512,1056]{1,0:T(8,128)}), f32[32,1056]{1,0:T(8,128)}) %reduce-scatter.2.cloned.1.call-update) | async-done | bytes 135184 | tf_op jit(solution)/shard_map/reduce_scatter | solution.py:38
  (63 shorter events, 27.8 us)
Async XLA Ops:
  11.1 79.2 %all-to-all-start = ((f32[16,32,4,1,256]{4,3,2,1,0:T(1,128)}), f32[16,32,4,1,256]{4,3,2,1,0:T(1,128)S(1)}, u32[]{:S(2)}, u32[]{:S(2)}) async-start(f32[16,32,4,1,256]{4,3,2,1,0:T(1,128)} %broadcast_in_dim.4), calls=%async_computation | async-start | bytes 4194304 | tf_op jit(solution)/shard_map/all_to_all | solution.py:9
  18.5 198.2 %all-gather.3.cloned.1.call-start = ((), (), s32[]{:S(2)}) async-start(), calls=%async_computation.5 | async-start | bytes 2228224 | tf_op jit(solution)/shard_map/all_gather | solution.py:88
  99.7 4.0 copy-start
  169.4 146.5 %all-gather.5.cloned.1.call-start = ((), (), s32[]{:S(2)}) async-start(), calls=%async_computation.6 | async-start | bytes 2785280 | tf_op jit(solution)/shard_map/all_gather | solution.py:92
  206.8 9.2 %copy-start.4 = (f32[32,6,1,256]{3,2,1,0:T(1,128)S(1)}, f32[32,6,1,256]{3,2,1,0:T(1,128)}, u32[]{:S(2)}) copy-start(f32[32,6,1,256]{3,2,1,0:T(1,128)} %param.9) | copy-start | bytes 589828
  216.7 13.7 %copy-start.2 = (f32[512,512]{1,0:T(8,128)}, f32[512,512]{1,0:T(8,128)S(1)}, u32[]{:S(2)}) copy-start(f32[512,512]{1,0:T(8,128)S(1)} %select_maximum_fusion) | copy-start | bytes 3145732
  279.3 167.4 %reduce-scatter.2.cloned.1.call-start = ((), (), s32[]{:S(2)}) async-start(), calls=%async_computation.7 | async-start | bytes 2506752 | tf_op jit(solution)/shard_map/reduce_scatter | solution.py:38
  356.7 2.2 copy-start.1
  358.8 7.0 %copy-start.3 = (f32[32,1024]{1,0:T(8,128)S(1)}, f32[32,1024]{1,0:T(8,128)}, u32[]{:S(2)}) copy-start(f32[32,1024]{1,0:T(8,128)} %reduce_sum.18) | copy-start | bytes 393220
Sparse Core Ops, SparseCore 0:
  169.5 37.7 all-gather.2
  279.4 36.4 all-gather.4
  369.4 77.3 reduce-scatter.1
where the time goes:
time: 464 us; the launch traced here: 457 us
  blocking collectives  137 us (30%)
  waiting for transfers between devices  113 us (24%)
  other arithmetic  103 us (22%)
  matrix products  41.4 us (9%)
  local copies, waits for them, and re-layouts  40.7 us (9%)
  between operations  14.5 us (3%)
  starting transfers between devices  7.6 us (2%)
    all_to_all x2, blocking collectives, sum_at_owner(): lax.all_to_all(parts, axis, split_axis=0, concat_axis=0, tiled=True)  103 us
    reduce_scatter x1, waiting for transfers between devices, in_one_piece(): result = lax.psum_scatter(both, axis, scatter_dimension=dim, tiled=True)  76.6 us
    unnamed x3, other arithmetic  52.1 us
    all_gather x1, waiting for transfers between devices, per_device(): lax.all_gather(kept_cols, 'prow', axis=2, tiled=True).reshape(x_rows, -1)  36.6 us
    all_to_all x1, blocking collectives, per_device(): lax.all_to_all(head_cols.reshape(x_rows, col_blocks, lax.axis_size('pcol'...  33.8 us
    dot_general x6, matrix products, matmul_hi(): jnp.dot(left, right, precision=lax.Precision.HIGHEST, preferred_element_t...  29.3 us
    unnamed x19, local copies, waits for them, and re-layouts  22.7 us
    another operation x2, other arithmetic, invert_diag(): lax.linalg.triangular_solve(diag_bottom, identity, left_side=True, lower=...  20.7 us
  transfers between devices with their start and end apart: 4, of which 2 were waited for; matrix products, arithmetic and copies ran while one was open for 26% of the time, Pallas kernels for 0%

commit v1 on v0

--- a/solution.py
+++ b/solution.py
@@ -89,7 +89,7 @@
     x_local = sum_at_owner(product + side_term, "pcol", 0)
     x_slab = x_local.reshape(x_rows, h_blocks, 1, block_size)
     kept_cols = x_slab[:, : prev_blocks + 1]
-    widened = lax.all_gather(kept_cols, "prow", axis=2, tiled=True).reshape(x_rows, -1)
+    widened = jnp.concatenate(lax.all_gather(kept_cols, "prow"), axis=2).reshape(x_rows, -1)
     prev_rows = prev_blocks * block_size * lax.axis_size("prow")
     head_cols = widened[:, :prev_rows]
     tail_cols = widened[:, prev_rows : prev_rows + slab_rows]

time: 464 us -> 466 us (level)
    unnamed x19 -> x21, local copies, waits for them, and re-layouts: 22.7 us -> 20.3 us
where the time goes in v1:
time: 466 us; the launch traced here: 459 us
  blocking collectives  137 us (29%)
  waiting for transfers between devices  114 us (24%)
  other arithmetic  103 us (22%)
  local copies, waits for them, and re-layouts  41.8 us (9%)
  matrix products  41.4 us (9%)
  between operations  14.5 us (3%)
  starting transfers between devices  7.6 us (2%)
    all_to_all x2, blocking collectives, sum_at_owner(): lax.all_to_all(parts, axis, split_axis=0, concat_axis=0, tiled=True)  103 us
    reduce_scatter x1, waiting for transfers between devices, in_one_piece(): result = lax.psum_scatter(both, axis, scatter_dimension=dim, tiled=True)  77.5 us
    unnamed x3, other arithmetic  52.1 us
    all_gather x1, waiting for transfers between devices, per_device(): lax.all_gather(kept_cols, 'prow')  36.6 us
    all_to_all x1, blocking collectives, per_device(): lax.all_to_all(head_cols.reshape(x_rows, col_blocks, lax.axis_size('pcol'...  33.8 us
    dot_general x6, matrix products, matmul_hi(): jnp.dot(left, right, precision=lax.Precision.HIGHEST, preferred_element_t...  29.3 us
    another operation x2, other arithmetic, invert_diag(): lax.linalg.triangular_solve(diag_bottom, identity, left_side=True, lower=...  20.7 us
    unnamed x21, local copies, waits for them, and re-layouts  20.3 us
  transfers between devices with their start and end apart: 4, of which 2 were waited for; matrix products, arithmetic and copies ran while one was open for 26% of the time, Pallas kernels for 0%

profile of v1, /device:TPU:2, one launch (start us, length us, event | category | flops | bytes accessed | tf_op | source)
XLA Modules:
  0.0 459.0 jit_solution(12524832312606488522)
XLA Ops:
  8.1 2.9 broadcast_in_dim.4
  11.0 7.5 %all-to-all-start = ((f32[16,32,4,1,256]{4,3,2,1,0:T(1,128)}), f32[16,32,4,1,256]{4,3,2,1,0:T(1,128)S(1)}, u32[]{:S(2)}, u32[]{:S(2)}) async-start(f32[16,32,4,1,256]{4,3,2,1,0:T(1,128)} %broadcast_in_dim.4), calls=%async_computation | async-start | bytes 4194304 | tf_op jit(solution)/shard_map/all_to_all | solution.py:9
  19.8 3.9 while.4
  23.7 19.7 %custom-call.4 = f32[2,128,128]{1,2,0:T(8,128)S(1)} custom-call(f32[2,128,128]{2,1,0:T(8,128)S(1)} %get-tuple-element.18), custom_call_target="InvertDiagBlocksLowerTriangular" | custom-call | tf_op jit(solution)/shard_map/triangular_solve/custom-call.1 | solution.py:61
  43.4 4.0 while.5
  47.4 19.7 %custom-call.5 = f32[2,128,128]{1,2,0:T(8,128)S(1)} custom-call(f32[2,128,128]{2,1,0:T(8,128)S(1)} %get-tuple-element.19), custom_call_target="InvertDiagBlocksLowerTriangular" | custom-call | tf_op jit(solution)/shard_map/triangular_solve/custom-call.1 | solution.py:62
  67.1 14.2 %reduce.1 = f32[4,256,4,256]{3,2,1,0:T(4,128)} reduce(f32[4,1,256,4,1,256]{5,4,3,2,1,0:T(1,128)} %param.7, f32[]{:T(128)} %constant.47), dimensions={1,4}, to_apply=%param.7.reduce_sub_computation | reduce | bytes 8388612 | tf_op args[0]
  81.4 5.1 %copy.25 = f32[128,8,4,256]{3,1,2,0:T(8,128)} copy(f32[128,8,4,256]{3,2,1,0:T(4,128)} %bitcast.86) | data formatting | bytes 8388608
  90.3 7.4 %reduce = f32[16,32,4,256]{3,2,1,0:T(4,128)} reduce(f32[16,32,4,1,256]{4,3,2,1,0:T(1,128)S(1)} %all-to-all-done, f32[]{:T(128)} %constant.47), dimensions={3}, to_apply=%all_to_all.20.reduce_sub_computation | reduce | bytes 4194308 | tf_op jit(solution)/shard_map/all_to_all | solution.py:9
  97.7 2.1 copy.24
  99.8 4.0 fusion.22
  103.7 6.9 %convolution_negate_fusion = f32[512,1024]{1,0:T(8,128)S(1)} fusion(f32[512,1024]{1,0:T(8,128)S(1)} %fusion.22, f32[1024,1024]{1,0:T(8,128)S(1)} %bitcast.81), kind=kOutput, calls=%fused_computation.7 | convolution fusion | flops 6442975232 | bytes 8388608 | tf_op jit(solution)/shard_map/dot_general | solution.py:43
  110.7 58.0 %all_to_all.31 = f32[16,32,1024]{2,1,0:T(8,128)S(1)} all-to-all(f32[16,32,1024]{2,1,0:T(8,128)S(1)} %bitcast.94), channel_id=1, replica_groups=mesh['prow'=16,'pcol'=16] {'prow'}, dimensions={0} | all-to-all | bytes 4194304 | tf_op jit(solution)/shard_map/all_to_all | solution.py:31
  169.5 37.4 %reduce.2 = f32[4,256,6,256]{3,2,1,0:T(8,128)} reduce(f32[4,1,256,6,1,256]{5,4,3,2,1,0:T(1,128)} %param.8, f32[]{:T(128)} %constant.47), dimensions={1,4}, to_apply=%param.8.reduce_sub_computation | reduce | bytes 12582916 | tf_op args[1]
  206.9 9.2 %copy.26 = f32[128,8,6,256]{3,1,2,0:T(8,128)} copy(f32[128,8,6,256]{3,2,1,0:T(8,128)} %bitcast.83) | data formatting | bytes 12582912
  216.8 13.7 %fusion.25 = f32[512,1536]{1,0:T(8,128)S(1)} fusion(f32[512,1024]{1,0:T(8,128)} %all-gather.4.cloned.1.call-done, f32[1024,1536]{1,0:T(8,128)} %bitcast.95), kind=kOutput, calls=%fused_computation.48 | convolution fusion | flops 9663676416 | bytes 11534336 | tf_op jit(solution)/shard_map/dot_general | solution.py:43
  230.5 2.8 convolution_add_fusion
  233.3 45.1 %all_to_all.32 = f32[16,32,1536]{2,1,0:T(8,128)S(1)} all-to-all(f32[16,32,1536]{2,1,0:T(8,128)S(1)} %bitcast.87), channel_id=1, replica_groups=mesh['prow'=16,'pcol'=16] {'pcol'}, dimensions={0} | all-to-all | bytes 6291456 | tf_op jit(solution)/shard_map/all_to_all | solution.py:31
  279.6 36.6 %all-gather.6.cloned.1.call-done = f32[512,5,1,256]{3,2,1,0:T(1,128)} async-done(((f32[32,5,1,256]{3,2,1,0:T(1,128)}), f32[512,5,1,256]{3,2,1,0:T(1,128)}) %all-gather.6.cloned.1.call-update) | async-done | bytes 2621456 | tf_op jit(solution)/shard_map/all_gather | solution.py:92
  316.2 3.3 copy.32
  324.8 33.8 %all_to_all.30 = f32[32,4,16,256]{3,1,0,2:T(4,128)S(1)} all-to-all(f32[32,4,16,256]{3,1,0,2:T(4,128)S(1)} %copy.18), channel_id=1, replica_groups=mesh['prow'=16,'pcol'=16] {'pcol'}, dimensions={2} | all-to-all | bytes 4194304 | tf_op jit(solution)/shard_map/all_to_all | solution.py:96
  360.8 7.0 %fusion.26 = f32[512,1024]{1,0:T(8,128)S(1)} fusion(f32[512,1024]{1,0:T(8,128)S(1)} %bitcast.84, f32[1024,1024]{1,0:T(8,128)S(1)} %bitcast.82), kind=kOutput, calls=%fused_computation.49 | convolution fusion | flops 6442450944 | bytes 8388608 | tf_op jit(solution)/shard_map/dot_general | solution.py:47
  367.8 1.8 fusion.27
  371.2 77.5 %reduce-scatter.2.cloned.1.call-done = f32[32,1056]{1,0:T(8,128)} async-done(((f32[512,1056]{1,0:T(8,128)}), f32[32,1056]{1,0:T(8,128)}) %reduce-scatter.2.cloned.1.call-update) | async-done | bytes 135184 | tf_op jit(solution)/shard_map/reduce_scatter | solution.py:38
  (67 shorter events, 29.0 us)
Async XLA Ops:
  11.0 79.3 %all-to-all-start = ((f32[16,32,4,1,256]{4,3,2,1,0:T(1,128)}), f32[16,32,4,1,256]{4,3,2,1,0:T(1,128)S(1)}, u32[]{:S(2)}, u32[]{:S(2)}) async-start(f32[16,32,4,1,256]{4,3,2,1,0:T(1,128)} %broadcast_in_dim.4), calls=%async_computation | async-start | bytes 4194304 | tf_op jit(solution)/shard_map/all_to_all | solution.py:9
  18.5 198.3 %all-gather.4.cloned.1.call-start = ((), (), s32[]{:S(2)}) async-start(), calls=%async_computation.5 | async-start | bytes 2228224 | tf_op jit(solution)/shard_map/all_gather | solution.py:88
  99.8 4.0 copy-start
  169.5 146.7 %all-gather.6.cloned.1.call-start = ((), (), s32[]{:S(2)}) async-start(), calls=%async_computation.7 | async-start | bytes 2785280 | tf_op jit(solution)/shard_map/all_gather | solution.py:92
  206.9 9.2 %copy-start.6 = (f32[32,6,1,256]{3,2,1,0:T(1,128)S(1)}, f32[32,6,1,256]{3,2,1,0:T(1,128)}, u32[]{:S(2)}) copy-start(f32[32,6,1,256]{3,2,1,0:T(1,128)} %param.9) | copy-start | bytes 589828
  216.8 13.7 %copy-start.3 = (f32[512,512]{1,0:T(8,128)}, f32[512,512]{1,0:T(8,128)S(1)}, u32[]{:S(2)}) copy-start(f32[512,512]{1,0:T(8,128)S(1)} %select_maximum_fusion) | copy-start | bytes 3145732
  278.8 40.7 %copy-start.5 = (f32[32,6,1,256]{3,2,1,0:T(1,128)}, f32[32,6,1,256]{3,2,1,0:T(1,128)S(1)}, u32[]{:S(2)}) copy-start(f32[32,6,1,256]{3,2,1,0:T(1,128)S(1)} %reshape.49) | copy-start | bytes 589828
  279.6 169.1 %reduce-scatter.2.cloned.1.call-start = ((), (), s32[]{:S(2)}) async-start(), calls=%async_computation.6 | async-start | bytes 2506752 | tf_op jit(solution)/shard_map/reduce_scatter | solution.py:38
  321.2 1.6 slice-start
  358.6 2.2 copy-start.1
  360.8 7.0 %copy-start.4 = (f32[32,1024]{1,0:T(8,128)S(1)}, f32[32,1024]{1,0:T(8,128)}, u32[]{:S(2)}) copy-start(f32[32,1024]{1,0:T(8,128)} %reduce_sum.18) | copy-start | bytes 393220
  371.2 79.2 %copy-start.2 = (f32[32,20480]{1,0:T(8,128)S(1)}, f32[32,20480]{1,0:T(8,128)}, u32[]{:S(2)}) copy-start(f32[32,20480]{1,0:T(8,128)} %reshape_reshape.7) | copy-start | bytes 7864324
Sparse Core Ops, SparseCore 0:
  169.6 37.7 all-gather.3
  279.7 36.4 all-gather.5
  371.3 77.3 reduce-scatter.1
